TPU v7x, 32 devices: a whole 2x2x4 slice. The times are simulated.
32 devices in a mesh: freq: 32 (over z, y, x, core).
Axes of the slice: x: 2, y: 2, z: 4, core: 2. Of those that a mesh axis runs over, the one named last changes fastest.
Arguments:
- pulses: float32 [1, 2, 30, 65536], P(None, None, None, 'freq'), may hold values from -4 to 4
- coupling: float32 [2, 30, 30, 65536], P(None, None, None, 'freq'), may hold values from -0.4 to 0.4
- dispersion_terms: float32 [3, 30], replicated, may hold values from -3 to 3
- kerr_gain: float32 [30], replicated, may hold values from 0.01 to 0.08
Outputs:
- evolved: float32 [1, 2, 30, 65536], P(None, None, None, 'freq')
All inputs are finite; a program needn't handle non-finite values.
Results may differ from a plain program's by a relative error of at most 0.00027.
Values sent between devices are 32-bit elements; how exact they have to be, the bound alone decides.
A program may use at most 128 MiB of HBM per device.

v0:
```python
import functools

import jax
import jax.numpy as jnp
import numpy as np
from jax import lax
from jax.experimental import pallas as pl
from jax.experimental.pallas import tpu as pltpu
from jax.sharding import PartitionSpec as P

STEPS = 2


HIGHEST = lax.Precision.HIGHEST


def angle_table(first, second, modulus, orient):
    turns = first[:, None] * second[None, :] % modulus
    radians = turns.astype(jnp.float32) * (2.0 * jnp.pi / modulus)
    return (jnp.cos(radians), orient * jnp.sin(radians))


def rotate(real_part, imag_part, cosine, sine):
    return (real_part * cosine - imag_part * sine, real_part * sine + imag_part * cosine)


def transform(stacked, cosine, sine):
    real_part = stacked[:, 0]
    imag_part = stacked[:, 1]
    out_real = jnp.matmul(real_part, cosine, precision=HIGHEST) - jnp.matmul(
        imag_part, sine, precision=HIGHEST
    )
    out_imag = jnp.matmul(real_part, sine, precision=HIGHEST) + jnp.matmul(
        imag_part, cosine, precision=HIGHEST
    )
    return jnp.stack((out_real, out_imag), axis=1)


def nonlinear_phase(stacked, kerr_gain):
    magnitude = stacked[:, 0] ** 2 + stacked[:, 1] ** 2
    total_power = jnp.sum(magnitude, axis=1, keepdims=True)
    gains = kerr_gain.reshape((1, -1) + (1,) * (magnitude.ndim - 2))
    angles = gains * (2.0 * total_power - magnitude)
    real_part, imag_part = rotate(stacked[:, 0], stacked[:, 1], jnp.cos(angles), jnp.sin(angles))
    return jnp.stack((real_part, imag_part), axis=1)


def per_device(pulses, coupling, dispersion_terms, kerr_gain):
    shards = lax.axis_size("freq")
    device = lax.axis_index("freq")
    mode_count = pulses.shape[2]
    local_count = pulses.shape[3]
    groups = local_count // shards
    total_count = local_count * shards
    column_index = jnp.arange(shards, dtype=jnp.int32)
    row_index = jnp.arange(local_count, dtype=jnp.int32)
    short_cos, short_sin = angle_table(column_index, column_index, shards, -1.0)
    inverse_short_cos, inverse_short_sin = angle_table(column_index, column_index, shards, 1.0)
    long_cos, long_sin = angle_table(row_index, row_index, local_count, -1.0)
    inverse_long_cos, inverse_long_sin = angle_table(row_index, row_index, local_count, 1.0)
    sample_rows = jnp.arange(groups, dtype=jnp.int32) * shards + device
    twist_cos, twist_sin = angle_table(sample_rows, column_index, total_count, -1.0)
    untwist_cos, untwist_sin = angle_table(row_index, jnp.reshape(device, (1,)), total_count, 1.0)
    untwist_cos = untwist_cos.reshape(-1)
    untwist_sin = untwist_sin.reshape(-1)
    bins = device + shards * row_index
    signed_bin = jnp.where(bins < total_count // 2, bins, bins - total_count).astype(jnp.float32)
    angular = signed_bin / (total_count // 2)
    dispersion = (
        dispersion_terms[0][:, None] * angular
        + dispersion_terms[1][:, None] * angular**2 / 2
        + dispersion_terms[2][:, None] * angular**3 / 6
    )
    spread_cos = jnp.cos(dispersion)
    spread_sin = jnp.sin(dispersion)
    identity = jnp.eye(mode_count, dtype=jnp.float32)[:, :, None]
    mixing_real = coupling[0] + identity
    mixing_imag = coupling[1]
    blocks = pulses.reshape(pulses.shape[0], 2, mode_count, groups, shards)
    columns = lax.all_to_all(blocks, "freq", split_axis=4, concat_axis=4, tiled=True)
    for repeat in range(STEPS):
        spectral = transform(columns, short_cos, short_sin)
        forward_real_part, forward_imag_part = rotate(
            spectral[:, 0], spectral[:, 1], twist_cos, twist_sin
        )
        evolve_rows = lax.all_to_all(
            jnp.stack((forward_real_part, forward_imag_part), axis=1),
            "freq",
            split_axis=4,
            concat_axis=4,
            tiled=True,
        )
        flat = evolve_rows.reshape(evolve_rows.shape[0], 2, mode_count, local_count)
        spectrum = transform(flat, long_cos, long_sin)
        spec_real = spectrum[:, 0]
        spec_imag = spectrum[:, 1]
        mixed_real = jnp.einsum(
            "nmk,bmk->bnk", mixing_real, spec_real, precision=HIGHEST
        ) - jnp.einsum("nmk,bmk->bnk", mixing_imag, spec_imag, precision=HIGHEST)
        mixed_imag = jnp.einsum(
            "nmk,bmk->bnk", mixing_real, spec_imag, precision=HIGHEST
        ) + jnp.einsum("nmk,bmk->bnk", mixing_imag, spec_real, precision=HIGHEST)
        real_part, imag_part = rotate(mixed_real, mixed_imag, spread_cos, spread_sin)
        inverted = transform(
            jnp.stack((real_part, imag_part), axis=1), inverse_long_cos, inverse_long_sin
        )
        real_part, imag_part = rotate(inverted[:, 0], inverted[:, 1], untwist_cos, untwist_sin)
        moved = jnp.stack((real_part, imag_part), axis=1).reshape(evolve_rows.shape)
        columns = nonlinear_phase(
            transform(
                lax.all_to_all(moved, "freq", split_axis=4, concat_axis=4, tiled=True),
                inverse_short_cos,
                inverse_short_sin,
            )
            * (1.0 / total_count),
            kerr_gain,
        )
    returned = lax.all_to_all(columns, "freq", split_axis=4, concat_axis=4, tiled=True)
    return returned.reshape(columns.shape[0], 2, mode_count, local_count)


LANES = 128
HALF = LANES // 2
SUB = 8


def low_lanes(shape):
    return lax.broadcasted_iota(jnp.int32, shape, len(shape) - 1) < HALF


def swap(x):
    return pltpu.roll(x, HALF, 1)


def sign_row(rows):
    return jnp.where(low_lanes((rows, LANES)), -1.0, 1.0).astype(jnp.float32)


def times_root(x, index, count, orient, sgn):
    eighth = 8 * index
    if index == 0:
        return x
    if eighth == 2 * count:
        return swap(x) * (sgn * orient)
    angle = 2.0 * np.pi * index / count
    return x * float(np.cos(angle)) + swap(x) * (sgn * float(orient * np.sin(angle)))


def short_fft(items, orient, sgn):
    count = len(items)
    if count == 1:
        return items
    even = short_fft(items[0::2], orient, sgn)
    odd = short_fft(items[1::2], orient, sgn)
    turned = [times_root(v, k, count, orient, sgn) for k, v in enumerate(odd)]
    return [e + t for e, t in zip(even, turned)] + [e - t for e, t in zip(even, turned)]


def packed_mul(x, cosine, signed_sine):
    return x * cosine + swap(x) * signed_sine


def split_constant(value, pieces, bits):
    parts = []
    for _ in range(pieces - 1):
        exponent = np.floor(np.log2(value))
        unit = 2.0 ** (exponent - bits + 1)
        part = np.floor(value / unit) * unit
        parts.append(float(part))
        value -= part
    return parts + [float(value)]


HALF_PI = split_constant(np.pi / 2, 4, 8)


def sine_cosine(theta):
    turns = jnp.floor(theta * float(2 / np.pi) + 0.5)
    rest = theta
    for part in HALF_PI:
        rest = rest - turns * part
    square = rest * rest
    sine = rest + rest * square * (
        -1.6666654611e-1 + square * (8.3321608736e-3 - square * 1.9515295891e-4)
    )
    cosine = 1.0 - 0.5 * square + square * square * (
        4.166664568298827e-2 + square * (-1.388731625493765e-3 + square * 2.443315711809948e-5)
    )
    quadrant = turns.astype(jnp.int32) & 3
    crossed = (quadrant & 1) == 1
    out_sine = jnp.where(crossed, cosine, sine)
    out_cosine = jnp.where(crossed, sine, cosine)
    out_sine = jnp.where(quadrant >= 2, -out_sine, out_sine)
    out_cosine = jnp.where((quadrant == 1) | (quadrant == 2), -out_cosine, out_cosine)
    return out_sine, out_cosine


def exchange_kernel(count, modes, x_ref, out_ref, send_sem, recv_sem, local_sem):
    me = lax.axis_index("freq")
    barrier = pltpu.get_barrier_semaphore()
    rows = x_ref.shape[1]
    if rows > modes:
        spare = pl.ds(rows - SUB, SUB)
        out_ref[:, spare, :] = jnp.zeros((count, SUB, x_ref.shape[2]), x_ref.dtype)

    def greet(k, carry):
        pl.semaphore_signal(
            barrier, inc=1, device_id=((me + k) % count,), device_id_type=pl.DeviceIdType.MESH
        )
        return carry

    lax.fori_loop(1, count, greet, 0)
    own = pltpu.make_async_copy(
        x_ref.at[me, pl.ds(0, modes)], out_ref.at[me, pl.ds(0, modes)], local_sem
    )
    own.start()
    pl.semaphore_wait(barrier, count - 1)

    def copy(k, slot):
        peer = (me + k) % count
        return pltpu.make_async_remote_copy(
            src_ref=x_ref.at[peer, pl.ds(0, modes)],
            dst_ref=out_ref.at[slot, pl.ds(0, modes)],
            send_sem=send_sem.at[k],
            recv_sem=recv_sem.at[k],
            device_id=(peer,),
            device_id_type=pl.DeviceIdType.MESH,
        )

    def send(j, carry):
        copy(count // 2 + (j // 2) * (1 - 2 * (j % 2)), me).start()
        return carry

    def drain(k, carry):
        copy(k, (me - k + count) % count).wait_recv()
        return carry

    def finish(k, carry):
        copy(k, me).wait_send()
        return carry

    lax.fori_loop(1, count, send, 0)
    own.wait()
    lax.fori_loop(1, count, drain, 0)
    lax.fori_loop(1, count, finish, 0)


def exchange(x, modes):
    count = x.shape[0]
    return pl.pallas_call(
        functools.partial(exchange_kernel, count, modes),
        out_shape=jax.ShapeDtypeStruct(x.shape, x.dtype),
        in_specs=[pl.BlockSpec(memory_space=pltpu.VMEM)],
        out_specs=pl.BlockSpec(memory_space=pltpu.VMEM),
        scratch_shapes=[
            pltpu.SemaphoreType.DMA((count,)),
            pltpu.SemaphoreType.DMA((count,)),
            pltpu.SemaphoreType.DMA(()),
        ],
        compiler_params=pltpu.CompilerParams(collective_id=0, has_side_effects=True),
        name="exchange",
    )(x)


def column_kernel(inverse, forward, scale, x_ref, cos_ref, sin_ref, gain_ref, out_ref, field):
    count, rows = x_ref.shape[0], x_ref.shape[1]
    sgn = sign_row(SUB)

    def chunk(c):
        return pl.ds(pl.multiple_of(c * SUB, SUB), SUB)

    if inverse:

        def undo(c, carry):
            rows_of = chunk(c)
            items = [
                packed_mul(
                    x_ref[d, rows_of, :], cos_ref[d : d + 1, :] * scale, sin_ref[d : d + 1, :] * -scale
                )
                for d in range(count)
            ]
            for a, value in enumerate(short_fft(items, 1.0, sgn)):
                field[a, rows_of, :] = value
            return carry

        lax.fori_loop(0, rows // SUB, undo, 0)
        wide = sign_row(rows)
        target = field if forward else out_ref

        def kerr(a, carry):
            x = field[a]
            square = x * x
            magnitude = square + swap(square)
            power = jnp.sum(magnitude, axis=0, keepdims=True)
            sine, cosine = sine_cosine(gain_ref[...] * (2.0 * power - magnitude))
            target[a] = packed_mul(x, cosine, sine * wide)
            return carry

        lax.fori_loop(0, count, kerr, 0, unroll=2)
    if forward:
        source = field if inverse else x_ref

        def apply(c, carry):
            rows_of = chunk(c)
            items = short_fft([source[a, rows_of, :] for a in range(count)], -1.0, sgn)
            for d, value in enumerate(items):
                out_ref[d, rows_of, :] = packed_mul(value, cos_ref[d : d + 1, :], sin_ref[d : d + 1, :])
            return carry

        lax.fori_loop(0, rows // SUB, apply, 0)


def column_stage(x, twist_cos, twist_sin, gain, scale, inverse, forward):
    return pl.pallas_call(
        functools.partial(column_kernel, inverse, forward, scale),
        out_shape=jax.ShapeDtypeStruct(x.shape, x.dtype),
        in_specs=[pl.BlockSpec(memory_space=pltpu.VMEM)] * 4,
        out_specs=pl.BlockSpec(memory_space=pltpu.VMEM),
        scratch_shapes=[pltpu.VMEM(x.shape, jnp.float32)],
        name="column",
    )(x, twist_cos, twist_sin, gain)


def long_dft(x, weights):
    high = x.astype(jnp.bfloat16)
    low = (x - high.astype(jnp.float32)).astype(jnp.bfloat16)
    both = jnp.concatenate((high, low), axis=1)
    product = jnp.dot(both, weights, preferred_element_type=jnp.float32)
    return product[:, :LANES] + product[:, LANES:]


def row_kernel(
    x_ref, c_ref, spread_cos_ref, spread_sin_ref, tw_cos_ref, tw_sin_ref, fwd_ref, inv_ref,
    out_ref, spec, by_real, by_imag, total,
):
    step = pl.program_id(0)
    count, rows = x_ref.shape[0], x_ref.shape[1]
    group, modes, width = c_ref.shape[0], c_ref.shape[1], c_ref.shape[2]
    sgn = sign_row(SUB)
    low = low_lanes((rows, LANES))

    def chunk(c):
        return pl.ds(pl.multiple_of(c * SUB, SUB), SUB)

    @pl.when(step == 0)
    def _():
        total[...] = jnp.zeros_like(total)

        def lanes(q, carry):
            part = pl.ds(q * 4, 4)
            block = x_ref[part].reshape(4 * rows, LANES)
            spec[part] = long_dft(block, fwd_ref[...]).reshape(4, rows, LANES)
            return carry

        lax.fori_loop(0, count // 4, lanes, 0)

        def across(c, carry):
            rows_of = chunk(c)
            items = [
                packed_mul(spec[p, rows_of, :], tw_cos_ref[p : p + 1, :], tw_sin_ref[p : p + 1, :])
                for p in range(count)
            ]
            for j, value in enumerate(short_fft(items, -1.0, sgn)):
                spec[j, rows_of, :] = value
            return carry

        lax.fori_loop(0, rows // SUB, across, 0)

        for tile in range(width // 2):
            first, second = spec[2 * tile], spec[2 * tile + 1]
            real = jnp.where(low, first, swap(second))
            imag = jnp.where(low, swap(first), second)
            for part in range(2):
                by_real[pl.ds(2 * tile + part, rows, stride=width), :] = real
                by_imag[pl.ds(2 * tile + part, rows, stride=width), :] = imag

    odd = lax.broadcasted_iota(jnp.int32, (SUB, LANES), 0) % 2 == 1

    def mix(q, carry):
        with_real = [jnp.zeros((SUB, LANES), jnp.float32) for _ in range(group)]
        with_imag = [jnp.zeros((SUB, LANES), jnp.float32) for _ in range(group)]
        for m in range(modes):
            at = pl.ds(pl.multiple_of(m * width + q * SUB, SUB), SUB)
            real, imag = by_real[at, :], by_imag[at, :]
            for g in range(group):
                factor = c_ref[g, m, chunk(q), :]
                with_real[g] = with_real[g] + factor * real
                with_imag[g] = with_imag[g] + factor * imag
        for g in range(group):
            other = jnp.where(
                odd, pltpu.roll(with_imag[g], 1, 0), -pltpu.roll(with_imag[g], SUB - 1, 0)
            )
            at = pl.ds(pl.multiple_of((step * group + g) * width + q * SUB, SUB), SUB)
            total[at, :] = with_real[g] + other
        return carry

    lax.fori_loop(0, width // SUB, mix, 0)

    @pl.when(step == pl.num_programs(0) - 1)
    def _():
        for tile in range(width // 2):
            first, second = spec[2 * tile], spec[2 * tile + 1]
            at = pl.ds(tile * LANES, LANES)
            real = jnp.where(low, first, swap(second)) + total[pl.ds(2 * tile, rows, stride=width), :]
            imag = jnp.where(low, swap(first), second) + total[
                pl.ds(2 * tile + 1, rows, stride=width), :
            ]
            real, imag = rotate(real, imag, spread_cos_ref[:, at], spread_sin_ref[:, at])
            spec[2 * tile] = jnp.where(low, real, swap(imag))
            spec[2 * tile + 1] = jnp.where(low, swap(real), imag)

        def across(c, carry):
            rows_of = chunk(c)
            items = short_fft([spec[j, rows_of, :] for j in range(count)], 1.0, sgn)
            for p, value in enumerate(items):
                spec[p, rows_of, :] = packed_mul(
                    value, tw_cos_ref[p : p + 1, :], -tw_sin_ref[p : p + 1, :]
                )
            return carry

        lax.fori_loop(0, rows // SUB, across, 0)

        def lanes(q, carry):
            part = pl.ds(q * 4, 4)
            block = spec[part].reshape(4 * rows, LANES)
            out_ref[part] = long_dft(block, inv_ref[...]).reshape(4, rows, LANES)
            return carry

        lax.fori_loop(0, count // 4, lanes, 0)


def row_stage(x, coupling, spread_cos, spread_sin, tw_cos, tw_sin, fwd, inv):
    rows = x.shape[1]
    modes, width = coupling.shape[0], coupling.shape[2]
    group = max(g for g in range(1, 7) if modes % g == 0)
    whole = lambda array: pl.BlockSpec(array.shape, lambda t: (0,) * array.ndim)
    return pl.pallas_call(
        row_kernel,
        grid=(modes // group,),
        out_shape=jax.ShapeDtypeStruct(x.shape, x.dtype),
        in_specs=[
            whole(x),
            pl.BlockSpec((group, modes, width, LANES), lambda t: (t, 0, 0, 0)),
            whole(spread_cos),
            whole(spread_sin),
            whole(tw_cos),
            whole(tw_sin),
            whole(fwd),
            whole(inv),
        ],
        out_specs=whole(x),
        scratch_shapes=[
            pltpu.VMEM(x.shape, jnp.float32),
            pltpu.VMEM((rows * width, LANES), jnp.float32),
            pltpu.VMEM((rows * width, LANES), jnp.float32),
            pltpu.VMEM((rows * width, LANES), jnp.float32),
        ],
        compiler_params=pltpu.CompilerParams(dimension_semantics=("arbitrary",)),
        name="row",
    )(x, coupling, spread_cos, spread_sin, tw_cos, tw_sin, fwd, inv)


def packed_table(cosine, sine):
    xp = np if isinstance(cosine, np.ndarray) else jnp
    return (
        xp.concatenate((cosine, cosine), axis=1).astype(xp.float32),
        xp.concatenate((-sine, sine), axis=1).astype(xp.float32),
    )


def dft_weights(size, orient):
    index = np.arange(size)
    angle = orient * 2.0 * np.pi * (index[:, None] * index[None, :] % size) / size
    cosine, sine = np.cos(angle), np.sin(angle)
    full = np.block([[cosine, sine], [-sine, cosine]]).astype(np.float32)
    high = full.astype(jnp.bfloat16)
    low = (full - high.astype(np.float32)).astype(jnp.bfloat16)
    return np.block([[high, low], [high, np.zeros_like(low)]])


def packed_device(pulses, coupling, dispersion_terms, kerr_gain):
    shards = lax.axis_size("freq")
    device = lax.axis_index("freq")
    modes, local = pulses.shape[2], pulses.shape[3]
    groups = local // shards
    total = local * shards
    rows = -(-modes // SUB) * SUB
    pad = rows - modes

    shard_index = np.arange(shards)
    angle = -2.0 * np.pi * (shard_index[:, None] * np.arange(groups)[None, :] % local) / local
    tw_cos, tw_sin = packed_table(np.cos(angle), np.sin(angle))
    fwd, inv = dft_weights(groups, -1.0), dft_weights(groups, 1.0)
    samples = device + shards * jnp.arange(groups, dtype=jnp.int32)
    twist_cos, twist_sin = packed_table(
        *angle_table(jnp.arange(shards, dtype=jnp.int32), samples, total, -1.0)
    )
    gain = jnp.broadcast_to(jnp.pad(kerr_gain, (0, pad))[:, None], (rows, LANES))

    bins = device + shards * jnp.arange(local, dtype=jnp.int32)
    signed_bin = jnp.where(bins < total // 2, bins, bins - total).astype(jnp.float32)
    angular = signed_bin / (total // 2)
    terms = jnp.pad(dispersion_terms, ((0, 0), (0, pad)))
    dispersion = (
        terms[0][:, None] * angular
        + terms[1][:, None] * angular**2 / 2
        + terms[2][:, None] * angular**3 / 6
    )
    spread_cos, spread_sin = jnp.cos(dispersion), jnp.sin(dispersion)

    coupling = coupling.reshape(2, modes, modes, local // LANES, LANES).transpose(1, 2, 3, 0, 4)
    coupling = coupling.reshape(modes, modes, 2 * local // LANES, LANES)
    blocks = pulses.reshape(2, modes, groups, shards).transpose(3, 1, 0, 2)
    x = jnp.pad(blocks.reshape(shards, modes, 2 * groups), ((0, 0), (0, pad), (0, 0)))
    scale = 1.0 / total
    for repeat in range(STEPS):
        x = exchange(x, modes) if repeat == 0 else x
        if repeat == 0:
            x = column_stage(x, twist_cos, twist_sin, gain, scale, False, True)
        x = exchange(x, modes)
        x = row_stage(x, coupling, spread_cos, spread_sin, tw_cos, tw_sin, fwd, inv)
        x = exchange(x, modes)
        x = column_stage(x, twist_cos, twist_sin, gain, scale, True, repeat < STEPS - 1)
    x = exchange(x, modes)
    x = x[:, :modes].reshape(shards, modes, 2, groups).transpose(2, 1, 3, 0)
    return x.reshape(1, 2, modes, local)


def fits(shards, pulses):
    local = pulses.shape[3] // shards
    return (
        pulses.shape[0] == 1
        and shards & (shards - 1) == 0
        and shards >= 4
        and local == shards * HALF
    )


def solution(mesh):
    in_specs = (P(None, None, None, "freq"), P(None, None, None, "freq"), P(), P())
    out_specs = P(None, None, None, "freq")
    shards = mesh.shape["freq"]

    def run(pulses, coupling, dispersion_terms, kerr_gain):
        body = packed_device if fits(shards, pulses) else per_device
        return jax.shard_map(
            body, mesh=mesh, in_specs=in_specs, out_specs=out_specs, check_vma=False
        )(pulses, coupling, dispersion_terms, kerr_gain)

    return run
```

profile of v0, /device:TPU:0, one launch (start us, length us, event | category | flops | bytes accessed | tf_op | source)
XLA Modules:
  0.0 177.0 jit_solution(9133266202925647441)
XLA Ops:
  0.0 0.1 fusion.11
  0.1 0.7 pad_maximum_fusion
  0.8 0.7 pad.13
  1.4 0.7 broadcast_in_dim.2.gain_ref
  2.1 1.9 %reshape.43 = f32[2,30,64,32]{3,2,0,1:T(8,128)S(1)} reshape(f32[1,2,30,2048]{3,1,2,0:T(2,128)} %param.8) | data formatting | bytes 983040 | tf_op jit(solution)/shard_map/reshape | solution.py:513
  4.0 0.7 copy.13
  4.7 0.0 copy-start
  4.7 0.8 pad.12.x_ref
  5.6 21.4 %exchange.6.x_ref = f32[32,32,128]{2,1,0:T(8,128)} custom-call(f32[32,32,128]{2,1,0:T(8,128)} %pad.12.x_ref), custom_call_target="tpu_custom_call" | custom-call | tf_op jit(solution)/shard_map/exchange/pallas_call | solution.py:250
  27.0 3.5 %column.3.x_ref = f32[32,32,128]{2,1,0:T(8,128)} custom-call(f32[32,32,128]{2,1,0:T(8,128)} %exchange.6.x_ref, f32[32,128]{1,0:T(8,128)} %get-tuple-element.15.cos_ref, f32[32,128]{1,0:T(8,128)} %get-tuple-element.16.sin_ref, f32[32,128]{1,0:T(8,128)} %broadcast_in_dim.2.gain_ref), custom_call_target="tpu_custom_call" | custom-call | tf_op jit(solution)/shard_map/column/pallas_call | solution.py:314
  30.4 18.7 %exchange.7.x_ref = f32[32,32,128]{2,1,0:T(8,128)} custom-call(f32[32,32,128]{2,1,0:T(8,128)} %column.3.x_ref), custom_call_target="tpu_custom_call" | custom-call | tf_op jit(solution)/shard_map/exchange/pallas_call | solution.py:250
  49.2 0.0 copy-done
  49.2 1.9 %fusion = (f32[32,2048]{1,0:T(8,128)}, f32[32,2048]{1,0:T(8,128)}) fusion(f32[2048]{0:T(1024)S(1)} %get-tuple-element.14, f32[32]{0:T(128)S(1)} %get-tuple-element.9, f32[2048]{0:T(1024)S(1)} %fusion.13, f32[32]{0:T(128)S(1)} %get-tuple-element.8, f32[2048]{0:T(1024)S(1)} %get-tuple-element.13, f32[32]{0:T(128)S(1)} %get-tuple-element.7), kind=kLoop, calls=%fused_computation.1 | loop fusion | flops 458752 | bytes 549248 | tf_op jit(solution)/shard_map/sin | solution.py:509
  51.1 16.7 %row.2.x_ref = f32[32,32,128]{2,1,0:T(8,128)} custom-call(f32[32,32,128]{2,1,0:T(8,128)} %exchange.7.x_ref, f32[30,30,32,128]{3,2,1,0:T(8,128)} %bitcast.24, f32[32,2048]{1,0:T(8,128)} %get-tuple-element.6.spread_cos_ref, f32[32,2048]{1,0:T(8,128)} %get-tuple-element.5.spread_sin_ref, f32[32,128]{1,0:T(8,128)} %constant.51.clone.tw_cos_ref, ...), custom_call_target="tpu_custom_call" | custom-call | tf_op jit(solution)/shard_map/row/pallas_call | solution.py:437
  67.8 18.7 %exchange.8.x_ref = f32[32,32,128]{2,1,0:T(8,128)} custom-call(f32[32,32,128]{2,1,0:T(8,128)} %row.2.x_ref), custom_call_target="tpu_custom_call" | custom-call | tf_op jit(solution)/shard_map/exchange/pallas_call | solution.py:250
  86.5 7.3 %column.4.x_ref = f32[32,32,128]{2,1,0:T(8,128)} custom-call(f32[32,32,128]{2,1,0:T(8,128)} %exchange.8.x_ref, f32[32,128]{1,0:T(8,128)} %get-tuple-element.15.cos_ref, f32[32,128]{1,0:T(8,128)} %get-tuple-element.16.sin_ref, f32[32,128]{1,0:T(8,128)} %broadcast_in_dim.2.gain_ref), custom_call_target="tpu_custom_call" | custom-call | tf_op jit(solution)/shard_map/column/pallas_call | solution.py:314
  93.8 18.7 %exchange.9.x_ref = f32[32,32,128]{2,1,0:T(8,128)} custom-call(f32[32,32,128]{2,1,0:T(8,128)} %column.4.x_ref), custom_call_target="tpu_custom_call" | custom-call | tf_op jit(solution)/shard_map/exchange/pallas_call | solution.py:250
  112.6 16.7 %row.3.x_ref = f32[32,32,128]{2,1,0:T(8,128)} custom-call(f32[32,32,128]{2,1,0:T(8,128)} %exchange.9.x_ref, f32[30,30,32,128]{3,2,1,0:T(8,128)} %bitcast.25, f32[32,2048]{1,0:T(8,128)} %get-tuple-element.6.spread_cos_ref, f32[32,2048]{1,0:T(8,128)} %get-tuple-element.5.spread_sin_ref, f32[32,128]{1,0:T(8,128)} %constant.51.clone.tw_cos_ref, ...), custom_call_target="tpu_custom_call" | custom-call | tf_op jit(solution)/shard_map/row/pallas_call | solution.py:437
  129.3 18.7 %exchange.10.x_ref = f32[32,32,128]{2,1,0:T(8,128)} custom-call(f32[32,32,128]{2,1,0:T(8,128)} %row.3.x_ref), custom_call_target="tpu_custom_call" | custom-call | tf_op jit(solution)/shard_map/exchange/pallas_call | solution.py:250
  148.0 5.7 %column.5.x_ref = f32[32,32,128]{2,1,0:T(8,128)} custom-call(f32[32,32,128]{2,1,0:T(8,128)} %exchange.10.x_ref, f32[32,128]{1,0:T(8,128)} %get-tuple-element.15.cos_ref, f32[32,128]{1,0:T(8,128)} %get-tuple-element.16.sin_ref, f32[32,128]{1,0:T(8,128)} %broadcast_in_dim.2.gain_ref), custom_call_target="tpu_custom_call" | custom-call | tf_op jit(solution)/shard_map/column/pallas_call | solution.py:314
  153.8 18.7 %exchange.11 = f32[32,32,128]{2,1,0:T(8,128)} custom-call(f32[32,32,128]{2,1,0:T(8,128)} %column.5.x_ref), custom_call_target="tpu_custom_call" | custom-call | tf_op jit(solution)/shard_map/exchange/pallas_call | solution.py:250
  172.5 1.3 copy.15
  173.8 0.6 reshape.47
  174.4 0.8 copy.16
  175.2 1.8 %reshape.48 = f32[1,2,30,2048]{3,1,2,0:T(2,128)} reshape(f32[2,30,64,32]{3,2,0,1:T(8,128)S(1)} %copy.16) | data formatting | bytes 983040 | tf_op jit(solution)/shard_map/reshape | solution.py:526
  (4 shorter events, 0.0 us)
Async XLA Ops:
  4.7 44.5 %copy-start = (f32[3,30]{1,0:T(4,128)S(1)}, f32[3,30]{1,0:T(4,128)}, u32[]{:S(2)}) copy-start(f32[3,30]{1,0:T(4,128)} %param.10) | copy-start | bytes 1084
where the time goes:
time: 178 us; the launch traced here: 177 us
  Pallas kernels  165 us (93%)
  local copies, waits for them, and re-layouts  9.27 us (5%)
  other arithmetic  2.66 us (1%)
    pallas_call x6, Pallas kernels, exchange(): pl.pallas_call(functools.partial(exchange_kernel, count, modes), out_shap...  115 us
    pallas_call x2, Pallas kernels, row_stage(): pl.pallas_call(row_kernel, grid=(modes // group,), out_shape=jax.ShapeDty...  33.4 us
    pallas_call x3, Pallas kernels, column_stage(): pl.pallas_call(functools.partial(column_kernel, inverse, forward, scale),...  16.5 us

commit v1 on v0

--- a/solution.py
+++ b/solution.py
@@ -195,132 +195,6 @@
     return out_sine, out_cosine
 
 
-def exchange_kernel(count, modes, x_ref, out_ref, send_sem, recv_sem, local_sem):
-    me = lax.axis_index("freq")
-    barrier = pltpu.get_barrier_semaphore()
-    rows = x_ref.shape[1]
-    if rows > modes:
-        spare = pl.ds(rows - SUB, SUB)
-        out_ref[:, spare, :] = jnp.zeros((count, SUB, x_ref.shape[2]), x_ref.dtype)
-
-    def greet(k, carry):
-        pl.semaphore_signal(
-            barrier, inc=1, device_id=((me + k) % count,), device_id_type=pl.DeviceIdType.MESH
-        )
-        return carry
-
-    lax.fori_loop(1, count, greet, 0)
-    own = pltpu.make_async_copy(
-        x_ref.at[me, pl.ds(0, modes)], out_ref.at[me, pl.ds(0, modes)], local_sem
-    )
-    own.start()
-    pl.semaphore_wait(barrier, count - 1)
-
-    def copy(k, slot):
-        peer = (me + k) % count
-        return pltpu.make_async_remote_copy(
-            src_ref=x_ref.at[peer, pl.ds(0, modes)],
-            dst_ref=out_ref.at[slot, pl.ds(0, modes)],
-            send_sem=send_sem.at[k],
-            recv_sem=recv_sem.at[k],
-            device_id=(peer,),
-            device_id_type=pl.DeviceIdType.MESH,
-        )
-
-    def send(j, carry):
-        copy(count // 2 + (j // 2) * (1 - 2 * (j % 2)), me).start()
-        return carry
-
-    def drain(k, carry):
-        copy(k, (me - k + count) % count).wait_recv()
-        return carry
-
-    def finish(k, carry):
-        copy(k, me).wait_send()
-        return carry
-
-    lax.fori_loop(1, count, send, 0)
-    own.wait()
-    lax.fori_loop(1, count, drain, 0)
-    lax.fori_loop(1, count, finish, 0)
-
-
-def exchange(x, modes):
-    count = x.shape[0]
-    return pl.pallas_call(
-        functools.partial(exchange_kernel, count, modes),
-        out_shape=jax.ShapeDtypeStruct(x.shape, x.dtype),
-        in_specs=[pl.BlockSpec(memory_space=pltpu.VMEM)],
-        out_specs=pl.BlockSpec(memory_space=pltpu.VMEM),
-        scratch_shapes=[
-            pltpu.SemaphoreType.DMA((count,)),
-            pltpu.SemaphoreType.DMA((count,)),
-            pltpu.SemaphoreType.DMA(()),
-        ],
-        compiler_params=pltpu.CompilerParams(collective_id=0, has_side_effects=True),
-        name="exchange",
-    )(x)
-
-
-def column_kernel(inverse, forward, scale, x_ref, cos_ref, sin_ref, gain_ref, out_ref, field):
-    count, rows = x_ref.shape[0], x_ref.shape[1]
-    sgn = sign_row(SUB)
-
-    def chunk(c):
-        return pl.ds(pl.multiple_of(c * SUB, SUB), SUB)
-
-    if inverse:
-
-        def undo(c, carry):
-            rows_of = chunk(c)
-            items = [
-                packed_mul(
-                    x_ref[d, rows_of, :], cos_ref[d : d + 1, :] * scale, sin_ref[d : d + 1, :] * -scale
-                )
-                for d in range(count)
-            ]
-            for a, value in enumerate(short_fft(items, 1.0, sgn)):
-                field[a, rows_of, :] = value
-            return carry
-
-        lax.fori_loop(0, rows // SUB, undo, 0)
-        wide = sign_row(rows)
-        target = field if forward else out_ref
-
-        def kerr(a, carry):
-            x = field[a]
-            square = x * x
-            magnitude = square + swap(square)
-            power = jnp.sum(magnitude, axis=0, keepdims=True)
-            sine, cosine = sine_cosine(gain_ref[...] * (2.0 * power - magnitude))
-            target[a] = packed_mul(x, cosine, sine * wide)
-            return carry
-
-        lax.fori_loop(0, count, kerr, 0, unroll=2)
-    if forward:
-        source = field if inverse else x_ref
-
-        def apply(c, carry):
-            rows_of = chunk(c)
-            items = short_fft([source[a, rows_of, :] for a in range(count)], -1.0, sgn)
-            for d, value in enumerate(items):
-                out_ref[d, rows_of, :] = packed_mul(value, cos_ref[d : d + 1, :], sin_ref[d : d + 1, :])
-            return carry
-
-        lax.fori_loop(0, rows // SUB, apply, 0)
-
-
-def column_stage(x, twist_cos, twist_sin, gain, scale, inverse, forward):
-    return pl.pallas_call(
-        functools.partial(column_kernel, inverse, forward, scale),
-        out_shape=jax.ShapeDtypeStruct(x.shape, x.dtype),
-        in_specs=[pl.BlockSpec(memory_space=pltpu.VMEM)] * 4,
-        out_specs=pl.BlockSpec(memory_space=pltpu.VMEM),
-        scratch_shapes=[pltpu.VMEM(x.shape, jnp.float32)],
-        name="column",
-    )(x, twist_cos, twist_sin, gain)
-
-
 def long_dft(x, weights):
     high = x.astype(jnp.bfloat16)
     low = (x - high.astype(jnp.float32)).astype(jnp.bfloat16)
@@ -329,135 +203,285 @@
     return product[:, :LANES] + product[:, LANES:]
 
 
-def row_kernel(
-    x_ref, c_ref, spread_cos_ref, spread_sin_ref, tw_cos_ref, tw_sin_ref, fwd_ref, inv_ref,
-    out_ref, spec, by_real, by_imag, total,
+def mega_kernel(
+    count, modes, scale, x_ref, c_hbm, spread_cos_ref, spread_sin_ref, tw_cos_ref, tw_sin_ref,
+    twist_cos_ref, twist_sin_ref, gain_ref, fwd_ref, inv_ref, out_ref,
+    c_ref, recv, send, spec, by_real, by_imag, total, field, acc, send_sem, recv_sem, c_sem,
 ):
-    step = pl.program_id(0)
-    count, rows = x_ref.shape[0], x_ref.shape[1]
-    group, modes, width = c_ref.shape[0], c_ref.shape[1], c_ref.shape[2]
+    me = lax.axis_index("freq")
+    rows = x_ref.shape[1]
+    chunks = rows // SUB
+    last = modes - (chunks - 1) * SUB
+    width = c_ref.shape[2]
+    pitch = by_real.shape[0] // rows
     sgn = sign_row(SUB)
-    low = low_lanes((rows, LANES))
-
-    def chunk(c):
+    low = low_lanes((SUB, LANES))
+    odd = lax.broadcasted_iota(jnp.int32, (SUB, LANES), 0) % 2 == 1
+    exchanges = recv.shape[0]
+
+    def tile_rows(c):
         return pl.ds(pl.multiple_of(c * SUB, SUB), SUB)
 
-    @pl.when(step == 0)
-    def _():
-        total[...] = jnp.zeros_like(total)
-
-        def lanes(q, carry):
-            part = pl.ds(q * 4, 4)
-            block = x_ref[part].reshape(4 * rows, LANES)
-            spec[part] = long_dft(block, fwd_ref[...]).reshape(4, rows, LANES)
+    def by_size(c, fn):
+        if last == SUB:
+            fn(SUB)
+        else:
+            pl.when(c < chunks - 1)(lambda: fn(SUB))
+            pl.when(c == chunks - 1)(lambda: fn(last))
+
+    def remote(src, dst, ex, c, peer):
+        return pltpu.make_async_remote_copy(
+            src_ref=src,
+            dst_ref=dst,
+            send_sem=send_sem.at[ex],
+            recv_sem=recv_sem.at[ex, c],
+            device_id=(peer,),
+            device_id_type=pl.DeviceIdType.MESH,
+        )
+
+    def post(src, ex, c):
+        def sized(size):
+            at = pl.ds(pl.multiple_of(c * SUB, SUB), size)
+            recv[ex, me, at, :] = src[me, at, :]
+
+            def one(j, carry):
+                peer = (me + count // 2 + (j // 2) * (1 - 2 * (j % 2))) % count
+                remote(src.at[peer, at], recv.at[ex, me, at], ex, c, peer).start()
+                return carry
+
+            lax.fori_loop(1, count, one, 0)
+
+        by_size(c, sized)
+
+    def arrive(ex, c):
+        def sized(size):
+            at = pl.ds(pl.multiple_of(c * SUB, SUB), size)
+            part = recv.at[ex, pl.ds(0, count - 1), at]
+            remote(part, part, ex, c, (me + 1) % count).wait_recv()
+
+        by_size(c, sized)
+
+    def each(body):
+        def step(c, carry):
+            body(c)
             return carry
 
-        lax.fori_loop(0, count // 4, lanes, 0)
-
-        def across(c, carry):
-            rows_of = chunk(c)
-            items = [
-                packed_mul(spec[p, rows_of, :], tw_cos_ref[p : p + 1, :], tw_sin_ref[p : p + 1, :])
+        lax.fori_loop(0, chunks, step, 0)
+
+    if rows > modes:
+        spare = pl.ds(modes, rows - modes)
+        for ex in range(exchanges):
+            recv[ex, :, spare, :] = jnp.zeros((count, rows - modes, LANES), jnp.float32)
+    total[...] = jnp.zeros_like(total)
+
+    load = pltpu.make_async_copy(c_hbm, c_ref, c_sem)
+    load.start()
+    barrier = pltpu.get_barrier_semaphore()
+
+    def greet(k, carry):
+        pl.semaphore_signal(
+            barrier, inc=1, device_id=((me + k) % count,), device_id_type=pl.DeviceIdType.MESH
+        )
+        return carry
+
+    lax.fori_loop(1, count, greet, 0)
+    pl.semaphore_wait(barrier, count - 1)
+
+    each(lambda c: post(x_ref, 0, c))
+
+    def columns_out(source, dst, ex, c):
+        at = tile_rows(c)
+        items = short_fft([source[a, at, :] for a in range(count)], -1.0, sgn)
+        for d, value in enumerate(items):
+            dst[d, at, :] = packed_mul(value, twist_cos_ref[d : d + 1, :], twist_sin_ref[d : d + 1, :])
+        post(dst, ex, c)
+
+    def row_in(ex, c):
+        at = tile_rows(c)
+        block = recv[ex, :, at, :].reshape(count * SUB, LANES)
+        spec[...] = long_dft(block, fwd_ref[...]).reshape(count, SUB, LANES)
+        items = short_fft(
+            [
+                packed_mul(spec[p], tw_cos_ref[p : p + 1, :], tw_sin_ref[p : p + 1, :])
                 for p in range(count)
-            ]
-            for j, value in enumerate(short_fft(items, -1.0, sgn)):
-                spec[j, rows_of, :] = value
-            return carry
-
-        lax.fori_loop(0, rows // SUB, across, 0)
-
+            ],
+            -1.0,
+            sgn,
+        )
         for tile in range(width // 2):
-            first, second = spec[2 * tile], spec[2 * tile + 1]
+            first, second = items[2 * tile], items[2 * tile + 1]
             real = jnp.where(low, first, swap(second))
             imag = jnp.where(low, swap(first), second)
             for part in range(2):
-                by_real[pl.ds(2 * tile + part, rows, stride=width), :] = real
-                by_imag[pl.ds(2 * tile + part, rows, stride=width), :] = imag
-
-    odd = lax.broadcasted_iota(jnp.int32, (SUB, LANES), 0) % 2 == 1
-
-    def mix(q, carry):
-        with_real = [jnp.zeros((SUB, LANES), jnp.float32) for _ in range(group)]
-        with_imag = [jnp.zeros((SUB, LANES), jnp.float32) for _ in range(group)]
-        for m in range(modes):
-            at = pl.ds(pl.multiple_of(m * width + q * SUB, SUB), SUB)
-            real, imag = by_real[at, :], by_imag[at, :]
-            for g in range(group):
-                factor = c_ref[g, m, chunk(q), :]
-                with_real[g] = with_real[g] + factor * real
-                with_imag[g] = with_imag[g] + factor * imag
-        for g in range(group):
-            other = jnp.where(
-                odd, pltpu.roll(with_imag[g], 1, 0), -pltpu.roll(with_imag[g], SUB - 1, 0)
+                to = pl.ds(c * SUB * pitch + 2 * tile + part, SUB, stride=pitch)
+                by_real[to, :] = real
+                by_imag[to, :] = imag
+
+    def mix(c, size):
+        def body(q, carry):
+            def spot(index):
+                return pl.ds(pl.multiple_of(index * pitch + q * SUB, SUB), SUB)
+
+            with_real = [
+                jnp.where(odd, by_imag[spot(c * SUB + g), :], by_real[spot(c * SUB + g), :])
+                for g in range(size)
+            ]
+            with_imag = [jnp.zeros((SUB, LANES), jnp.float32) for _ in range(size)]
+            for m in range(modes):
+                real, imag = by_real[spot(m), :], by_imag[spot(m), :]
+                for g in range(size):
+                    factor = c_ref[c * SUB + g, m, tile_rows(q), :]
+                    with_real[g] = with_real[g] + factor * real
+                    with_imag[g] = with_imag[g] + factor * imag
+            for g in range(size):
+                other = jnp.where(
+                    odd, pltpu.roll(with_imag[g], 1, 0), -pltpu.roll(with_imag[g], SUB - 1, 0)
+                )
+                total[spot(g), :] = with_real[g] + other
+            return carry
+
+        lax.fori_loop(0, width // SUB, body, 0)
+
+    def row_out(dst, ex, c):
+        at = tile_rows(c)
+        by_size(c, lambda size: mix(c, size))
+        items = []
+        for tile in range(width // 2):
+            lanes = pl.ds(tile * LANES, LANES)
+            real, imag = rotate(
+                total[pl.ds(2 * tile, SUB, stride=pitch), :],
+                total[pl.ds(2 * tile + 1, SUB, stride=pitch), :],
+                spread_cos_ref[at, lanes],
+                spread_sin_ref[at, lanes],
             )
-            at = pl.ds(pl.multiple_of((step * group + g) * width + q * SUB, SUB), SUB)
-            total[at, :] = with_real[g] + other
-        return carry
-
-    lax.fori_loop(0, width // SUB, mix, 0)
-
-    @pl.when(step == pl.num_programs(0) - 1)
-    def _():
-        for tile in range(width // 2):
-            first, second = spec[2 * tile], spec[2 * tile + 1]
-            at = pl.ds(tile * LANES, LANES)
-            real = jnp.where(low, first, swap(second)) + total[pl.ds(2 * tile, rows, stride=width), :]
-            imag = jnp.where(low, swap(first), second) + total[
-                pl.ds(2 * tile + 1, rows, stride=width), :
-            ]
-            real, imag = rotate(real, imag, spread_cos_ref[:, at], spread_sin_ref[:, at])
-            spec[2 * tile] = jnp.where(low, real, swap(imag))
-            spec[2 * tile + 1] = jnp.where(low, swap(real), imag)
-
-        def across(c, carry):
-            rows_of = chunk(c)
-            items = short_fft([spec[j, rows_of, :] for j in range(count)], 1.0, sgn)
-            for p, value in enumerate(items):
-                spec[p, rows_of, :] = packed_mul(
-                    value, tw_cos_ref[p : p + 1, :], -tw_sin_ref[p : p + 1, :]
-                )
+            items.append(jnp.where(low, real, swap(imag)))
+            items.append(jnp.where(low, swap(real), imag))
+        for p, value in enumerate(short_fft(items, 1.0, sgn)):
+            spec[p] = packed_mul(value, tw_cos_ref[p : p + 1, :], -tw_sin_ref[p : p + 1, :])
+        block = spec[...].reshape(count * SUB, LANES)
+        dst[:, at, :] = long_dft(block, inv_ref[...]).reshape(count, SUB, LANES)
+        post(dst, ex, c)
+
+    def columns_in(ex, c):
+        at = tile_rows(c)
+        items = [
+            packed_mul(
+                recv[ex, d, at, :],
+                twist_cos_ref[d : d + 1, :] * scale,
+                twist_sin_ref[d : d + 1, :] * -scale,
+            )
+            for d in range(count)
+        ]
+        for a, value in enumerate(short_fft(items, 1.0, sgn)):
+            field[a, at, :] = value
+            acc[a] = acc[a] + value * value
+
+    def power():
+        def body(a, carry):
+            part = jnp.sum(acc[a], axis=0, keepdims=True)
+            acc[a] = jnp.broadcast_to(2.0 * (part + swap(part)), (SUB, LANES))
             return carry
 
-        lax.fori_loop(0, rows // SUB, across, 0)
-
-        def lanes(q, carry):
-            part = pl.ds(q * 4, 4)
-            block = spec[part].reshape(4 * rows, LANES)
-            out_ref[part] = long_dft(block, inv_ref[...]).reshape(4, rows, LANES)
+        lax.fori_loop(0, count, body, 0, unroll=4)
+
+    def kerr(target, c):
+        at = tile_rows(c)
+        gain = gain_ref[at, :]
+
+        def body(a, carry):
+            x = field[a, at, :]
+            square = x * x
+            magnitude = square + swap(square)
+            sine, cosine = sine_cosine(gain * (acc[a] - magnitude))
+            target[a, at, :] = packed_mul(x, cosine, sine * sgn)
             return carry
 
-        lax.fori_loop(0, count // 4, lanes, 0)
-
-
-def row_stage(x, coupling, spread_cos, spread_sin, tw_cos, tw_sin, fwd, inv):
-    rows = x.shape[1]
-    modes, width = coupling.shape[0], coupling.shape[2]
-    group = max(g for g in range(1, 7) if modes % g == 0)
-    whole = lambda array: pl.BlockSpec(array.shape, lambda t: (0,) * array.ndim)
+        lax.fori_loop(0, count, body, 0, unroll=4)
+
+    ex = 1
+    for repeat in range(STEPS):
+        dst = send.at[ex - 1]
+        if repeat == 0:
+
+            def begin(c):
+                arrive(0, c)
+                columns_out(recv.at[0], dst, ex, c)
+
+            each(begin)
+        else:
+            power()
+
+            def bend(c):
+                kerr(field, c)
+                columns_out(field, dst, ex, c)
+
+            each(bend)
+
+        def inward(c):
+            arrive(ex, c)
+            row_in(ex, c)
+
+        each(inward)
+        if repeat == 0:
+            load.wait()
+        ex += 1
+        each(lambda c: row_out(send.at[ex - 1], ex, c))
+        acc[...] = jnp.zeros_like(acc)
+
+        def collect(c):
+            arrive(ex, c)
+            columns_in(ex, c)
+
+        each(collect)
+        ex += 1
+    power()
+
+    def finish(c):
+        kerr(send.at[ex - 1], c)
+        post(send.at[ex - 1], ex, c)
+
+    each(finish)
+
+    def result(c):
+        arrive(ex, c)
+        out_ref[:, tile_rows(c), :] = recv[ex, :, tile_rows(c), :]
+
+    each(result)
+    for ex in range(exchanges):
+        sent = recv.at[ex, pl.ds(0, count - 1), pl.ds(0, modes)]
+        remote(sent, sent, ex, 0, (me + 1) % count).wait_send()
+
+
+def mega(x, coupling, spread_cos, spread_sin, tw_cos, tw_sin, twist_cos, twist_sin, gain, fwd, inv, modes, scale):
+    count, rows = x.shape[0], x.shape[1]
+    width = coupling.shape[2]
+    pitch = width + SUB
+    exchanges = 2 * STEPS + 2
+    chunks = rows // SUB
+    vmem = pl.BlockSpec(memory_space=pltpu.VMEM)
+    block = (count, rows, LANES)
     return pl.pallas_call(
-        row_kernel,
-        grid=(modes // group,),
+        functools.partial(mega_kernel, count, modes, scale),
         out_shape=jax.ShapeDtypeStruct(x.shape, x.dtype),
-        in_specs=[
-            whole(x),
-            pl.BlockSpec((group, modes, width, LANES), lambda t: (t, 0, 0, 0)),
-            whole(spread_cos),
-            whole(spread_sin),
-            whole(tw_cos),
-            whole(tw_sin),
-            whole(fwd),
-            whole(inv),
+        in_specs=[vmem, pl.BlockSpec(memory_space=pl.ANY)] + [vmem] * 9,
+        out_specs=vmem,
+        scratch_shapes=[
+            pltpu.VMEM(coupling.shape, jnp.float32),
+            pltpu.VMEM((exchanges,) + block, jnp.float32),
+            pltpu.VMEM((exchanges - 1,) + block, jnp.float32),
+            pltpu.VMEM((count, SUB, LANES), jnp.float32),
+            pltpu.VMEM((rows * pitch, LANES), jnp.float32),
+            pltpu.VMEM((rows * pitch, LANES), jnp.float32),
+            pltpu.VMEM((SUB * pitch, LANES), jnp.float32),
+            pltpu.VMEM(block, jnp.float32),
+            pltpu.VMEM((count, SUB, LANES), jnp.float32),
+            pltpu.SemaphoreType.DMA((exchanges,)),
+            pltpu.SemaphoreType.DMA((exchanges, chunks)),
+            pltpu.SemaphoreType.DMA(()),
         ],
-        out_specs=whole(x),
-        scratch_shapes=[
-            pltpu.VMEM(x.shape, jnp.float32),
-            pltpu.VMEM((rows * width, LANES), jnp.float32),
-            pltpu.VMEM((rows * width, LANES), jnp.float32),
-            pltpu.VMEM((rows * width, LANES), jnp.float32),
-        ],
-        compiler_params=pltpu.CompilerParams(dimension_semantics=("arbitrary",)),
-        name="row",
-    )(x, coupling, spread_cos, spread_sin, tw_cos, tw_sin, fwd, inv)
+        compiler_params=pltpu.CompilerParams(collective_id=0, has_side_effects=True),
+        name="mega",
+    )(x, coupling, spread_cos, spread_sin, tw_cos, tw_sin, twist_cos, twist_sin, gain, fwd, inv)
 
 
 def packed_table(cosine, sine):
@@ -513,15 +537,9 @@
     blocks = pulses.reshape(2, modes, groups, shards).transpose(3, 1, 0, 2)
     x = jnp.pad(blocks.reshape(shards, modes, 2 * groups), ((0, 0), (0, pad), (0, 0)))
     scale = 1.0 / total
-    for repeat in range(STEPS):
-        x = exchange(x, modes) if repeat == 0 else x
-        if repeat == 0:
-            x = column_stage(x, twist_cos, twist_sin, gain, scale, False, True)
-        x = exchange(x, modes)
-        x = row_stage(x, coupling, spread_cos, spread_sin, tw_cos, tw_sin, fwd, inv)
-        x = exchange(x, modes)
-        x = column_stage(x, twist_cos, twist_sin, gain, scale, True, repeat < STEPS - 1)
-    x = exchange(x, modes)
+    x = mega(
+        x, coupling, spread_cos, spread_sin, tw_cos, tw_sin, twist_cos, twist_sin, gain, fwd, inv, modes, scale
+    )
     x = x[:, :modes].reshape(shards, modes, 2, groups).transpose(2, 1, 3, 0)
     return x.reshape(1, 2, modes, local)
 

time: 178 us -> 105 us (0.59)
  Pallas kernels: 165 us -> 93.7 us
    pallas_call x11 -> x1, Pallas kernels: 165 us -> 93.7 us  [mega(): pl.pallas_call(functools.partial(mega_kernel, count, modes, scale), out_s...]
where the time goes in v1:
time: 105 us
  Pallas kernels  93.7 us (89%)
  local copies, waits for them, and re-layouts  8.63 us (8%)
  other arithmetic  2.67 us (3%)
    pallas_call x1, Pallas kernels, mega(): pl.pallas_call(functools.partial(mega_kernel, count, modes, scale), out_s...  93.7 us

profile of v1, /device:TPU:0, one launch (start us, length us, event | category | flops | bytes accessed | tf_op | source)
XLA Modules:
  0.0 105.1 jit_solution(6837212348102898935)
XLA Ops:
  0.0 1.9 %reshape.43 = f32[2,30,64,32]{3,2,0,1:T(8,128)S(1)} reshape(f32[1,2,30,2048]{3,1,2,0:T(2,128)} %param.8) | data formatting | bytes 983040 | tf_op jit(solution)/shard_map/reshape | solution.py:537
  1.9 0.0 copy-start
  1.9 0.0 copy-start.1
  1.9 0.7 copy.13
  2.6 0.8 pad.12.x_ref
  3.5 0.0 copy-done
  3.5 1.9 %fusion = (f32[32,2048]{1,0:T(8,128)}, f32[32,2048]{1,0:T(8,128)}) fusion(f32[2048]{0:T(1024)S(1)} %get-tuple-element.14, f32[32]{0:T(128)S(1)} %get-tuple-element.9, f32[2048]{0:T(1024)S(1)} %fusion.13, f32[32]{0:T(128)S(1)} %get-tuple-element.8, f32[2048]{0:T(1024)S(1)} %get-tuple-element.13, f32[32]{0:T(128)S(1)} %get-tuple-element.7), kind=kLoop, calls=%fused_computation.1 | loop fusion | flops 458752 | bytes 549248 | tf_op jit(solution)/shard_map/sin | solution.py:533
  5.4 0.1 fusion.11
  5.5 0.7 pad_maximum_fusion
  6.1 0.0 copy-done.1
  6.2 0.7 broadcast_in_dim.2.gain_ref
  6.8 93.7 %mega.1 = f32[32,32,128]{2,1,0:T(8,128)} custom-call(f32[32,32,128]{2,1,0:T(8,128)} %pad.12.x_ref, f32[30,30,32,128]{3,2,1,0:T(8,128)} %bitcast.24, f32[32,2048]{1,0:T(8,128)} %get-tuple-element.6.spread_cos_ref, f32[32,2048]{1,0:T(8,128)} %get-tuple-element.5.spread_sin_ref, f32[32,128]{1,0:T(8,128)} %constant.51.clone.tw_cos_ref, ...), custom_call_target="tpu_custom_call" | custom-call | tf_op jit(solution)/shard_map/mega/pallas_call | solution.py:463
  100.6 1.3 %copy.15 = f32[32,30,128]{2,0,1:T(8,128)S(1)} copy(f32[32,30,128]{2,1,0:T(8,128)} %bitcast.27) | data formatting | bytes 983040 | tf_op jit(solution)/shard_map/slice | solution.py:543
  101.9 0.6 reshape.47
  102.5 0.8 copy.16
  103.3 1.8 %reshape.48 = f32[1,2,30,2048]{3,1,2,0:T(2,128)} reshape(f32[2,30,64,32]{3,2,0,1:T(8,128)S(1)} %copy.16) | data formatting | bytes 983040 | tf_op jit(solution)/shard_map/reshape | solution.py:544
  (5 shorter events, 0.0 us)
Async XLA Ops:
  1.9 1.6 %copy-start = (f32[3,30]{1,0:T(4,128)S(1)}, f32[3,30]{1,0:T(4,128)}, u32[]{:S(2)}) copy-start(f32[3,30]{1,0:T(4,128)} %param.10) | copy-start | bytes 1084
  1.9 4.3 %copy-start.1 = (f32[30]{0:T(128)S(1)}, f32[30]{0:T(128)}, u32[]{:S(2)}) copy-start(f32[30]{0:T(128)} %param.11) | copy-start | bytes 364

commit v2 on v1

--- a/solution.py
+++ b/solution.py
@@ -122,6 +122,8 @@
 LANES = 128
 HALF = LANES // 2
 SUB = 8
+ROW = 16
+GROUPS = ((0, 1), (1, 3), (3, 4))
 
 
 def low_lanes(shape):
@@ -129,7 +131,7 @@
 
 
 def swap(x):
-    return pltpu.roll(x, HALF, 1)
+    return pltpu.roll(x, HALF, x.ndim - 1)
 
 
 def sign_row(rows):
@@ -203,63 +205,94 @@
     return product[:, :LANES] + product[:, LANES:]
 
 
+def trade(vectors, stride, shift):
+    lane = lax.broadcasted_iota(jnp.int32, (SUB, LANES), 1)
+    lower = (lane // shift) % 2 == 0
+    out = list(vectors)
+    for k in range(len(vectors)):
+        if (k // stride) % 2 == 0:
+            first, second = vectors[k], vectors[k + stride]
+            out[k] = jnp.where(lower, first, pltpu.roll(second, shift, 1))
+            out[k + stride] = jnp.where(lower, pltpu.roll(first, LANES - shift, 1), second)
+    return out
+
+
 def mega_kernel(
-    count, modes, scale, x_ref, c_hbm, spread_cos_ref, spread_sin_ref, tw_cos_ref, tw_sin_ref,
-    twist_cos_ref, twist_sin_ref, gain_ref, fwd_ref, inv_ref, out_ref,
-    c_ref, recv, send, spec, by_real, by_imag, total, field, acc, send_sem, recv_sem, c_sem,
+    count, modes, scale, groups, pulse_ref, c_hbm, terms_ref, gain_in, tw_cos_ref, tw_sin_ref,
+    fwd_ref, inv_ref, out_ref, c_ref, early, recv, late, send, spec, by_real, by_imag, total, field,
+    acc, spread_cos_ref, spread_sin_ref, twist_cos_ref, twist_sin_ref, gain_ref,
+    send_sem, recv_sem, c_sem,
 ):
     me = lax.axis_index("freq")
-    rows = x_ref.shape[1]
-    chunks = rows // SUB
-    last = modes - (chunks - 1) * SUB
+    chunks = recv.shape[2] // SUB
+    rows = recv.shape[2]
     width = c_ref.shape[2]
     pitch = by_real.shape[0] // rows
+    span = early.shape[0] // count
     sgn = sign_row(SUB)
     low = low_lanes((SUB, LANES))
     odd = lax.broadcasted_iota(jnp.int32, (SUB, LANES), 0) % 2 == 1
-    exchanges = recv.shape[0]
+    exchanges = recv.shape[0] + 1
 
     def tile_rows(c):
         return pl.ds(pl.multiple_of(c * SUB, SUB), SUB)
 
-    def by_size(c, fn):
-        if last == SUB:
-            fn(SUB)
-        else:
-            pl.when(c < chunks - 1)(lambda: fn(SUB))
-            pl.when(c == chunks - 1)(lambda: fn(last))
-
-    def remote(src, dst, ex, c, peer):
+    def block_of(ref):
+        return lambda peer, row, size: ref.at[peer, pl.ds(row, size)]
+
+    def flat_of(ref):
+        return lambda peer, row, size: ref.at[pl.ds(pl.multiple_of(peer * span + row, SUB), size)]
+
+    def landing(ex):
+        return flat_of(late) if ex == exchanges - 1 else block_of(recv.at[ex])
+
+    def remote(src, dst, ex, g, peer):
         return pltpu.make_async_remote_copy(
             src_ref=src,
             dst_ref=dst,
             send_sem=send_sem.at[ex],
-            recv_sem=recv_sem.at[ex, c],
+            recv_sem=recv_sem.at[ex, g],
             device_id=(peer,),
             device_id_type=pl.DeviceIdType.MESH,
         )
 
+    def extent(g):
+        start, end = groups[g]
+        return start * SUB, min(end * SUB, modes) - start * SUB
+
     def post(src, ex, c):
-        def sized(size):
-            at = pl.ds(pl.multiple_of(c * SUB, SUB), size)
-            recv[ex, me, at, :] = src[me, at, :]
-
-            def one(j, carry):
-                peer = (me + count // 2 + (j // 2) * (1 - 2 * (j % 2))) % count
-                remote(src.at[peer, at], recv.at[ex, me, at], ex, c, peer).start()
-                return carry
-
-            lax.fori_loop(1, count, one, 0)
-
-        by_size(c, sized)
+        dst = landing(ex)
+        for g, (_, end) in enumerate(groups):
+            row, size = extent(g)
+
+            def go(row=row, size=size, g=g):
+                dst(me, row, size)[...] = src(me, row, size)[...]
+
+                def one(j, carry):
+                    k = count - j
+                    peer = 0
+                    for b in range(count.bit_length() - 1):
+                        mine = (me // (1 << b)) % 2
+                        peer = peer + ((k // (1 << b) + mine) % 2) * (1 << b)
+                    remote(src(peer, row, size), dst(me, row, size), ex, g, peer).start()
+                    return carry
+
+                lax.fori_loop(1, count, one, 0)
+
+            pl.when(c == end - 1)(go)
 
     def arrive(ex, c):
-        def sized(size):
-            at = pl.ds(pl.multiple_of(c * SUB, SUB), size)
-            part = recv.at[ex, pl.ds(0, count - 1), at]
-            remote(part, part, ex, c, (me + 1) % count).wait_recv()
-
-        by_size(c, sized)
+        for g, (start, _) in enumerate(groups):
+            row, size = extent(g)
+
+            def go(row=row, size=size, g=g):
+                if ex == exchanges - 1:
+                    part = late.at[pl.ds(0, (count - 1) * size)]
+                else:
+                    part = recv.at[ex, pl.ds(0, count - 1), pl.ds(row, size)]
+                remote(part, part, ex, g, (me + 1) % count).wait_recv()
+
+            pl.when(c == start)(go)
 
     def each(body):
         def step(c, carry):
@@ -267,12 +300,6 @@
             return carry
 
         lax.fori_loop(0, chunks, step, 0)
-
-    if rows > modes:
-        spare = pl.ds(modes, rows - modes)
-        for ex in range(exchanges):
-            recv[ex, :, spare, :] = jnp.zeros((count, rows - modes, LANES), jnp.float32)
-    total[...] = jnp.zeros_like(total)
 
     load = pltpu.make_async_copy(c_hbm, c_ref, c_sem)
     load.start()
@@ -285,16 +312,99 @@
         return carry
 
     lax.fori_loop(1, count, greet, 0)
+    if rows > modes:
+        spare = pl.ds(modes, rows - modes)
+        for ex in range(exchanges - 1):
+            recv[ex, :, spare, :] = jnp.zeros((count, rows - modes, LANES), jnp.float32)
+    total[...] = jnp.zeros_like(total)
+
+    def unpack(q):
+        names = [min(4 * q + i, modes - 1) for i in range(4)]
+        pieces = [
+            pulse_ref[m, pl.ds(ri + 2 * SUB * half, SUB, stride=2), :]
+            for ri in range(2)
+            for m in names
+            for half in range(2)
+        ]
+        turned = jnp.concatenate(pieces, axis=0).T
+        for eb in range(count // SUB):
+            parts = [turned[gl * count + eb * SUB : gl * count + eb * SUB + SUB] for gl in range(4)]
+            parts = trade(trade(parts, 2, 2 * ROW), 1, ROW)
+            for i in range(4):
+                if 4 * q + i < modes:
+                    early[pl.ds(eb * SUB * span + 4 * q + i, SUB, stride=span), :] = parts[i]
+
+    def repack(q):
+        names = [min(4 * q + i, modes - 1) for i in range(4)]
+        pieces = [[] for _ in range(4)]
+        for eb in range(count // SUB):
+            parts = [late[pl.ds(eb * SUB * span + m, SUB, stride=span), :] for m in names]
+            parts = trade(trade(parts, 1, ROW), 2, 2 * ROW)
+            for gl in range(4):
+                pieces[gl].append(parts[gl])
+        turned = jnp.concatenate([p for piece in pieces for p in piece], axis=0).T
+        for ri in range(2):
+            for i in range(4):
+                if 4 * q + i < modes:
+                    for half in range(2):
+                        at = (ri * 4 + i) * ROW + half * SUB
+                        out_ref[4 * q + i, pl.ds(ri + 2 * SUB * half, SUB, stride=2), :] = turned[
+                            at : at + SUB
+                        ]
+
+    for q in range(2 * groups[0][1]):
+        unpack(q)
     pl.semaphore_wait(barrier, count - 1)
-
-    each(lambda c: post(x_ref, 0, c))
+    for c in range(chunks):
+        if c >= groups[0][1]:
+            unpack(2 * c)
+            unpack(2 * c + 1)
+        if c in [end - 1 for _, end in groups]:
+            post(flat_of(early), 0, c)
+
+    lane = lax.broadcasted_iota(jnp.int32, (SUB, LANES), 1)
+    line = lax.broadcasted_iota(jnp.int32, (SUB, LANES), 0)
+    place = lane % HALF
+    sample = me + count * (place % ROW * 4 + place // ROW)
+    total_count = count * count * HALF
+    for c in range(count // SUB):
+        turns = (line + c * SUB) * sample
+        sine, cosine = sine_cosine(turns.astype(jnp.float32) * (2.0 * np.pi / total_count))
+        twist_cos_ref[tile_rows(c), :] = cosine
+        twist_sin_ref[tile_rows(c), :] = sine * -sgn
+
+    def by_mode(read, c):
+        value = jnp.zeros((SUB, LANES), jnp.float32)
+        for r in range(min(SUB, modes - c * SUB)):
+            value = jnp.where(line == r, read(c * SUB + r), value)
+        return value
+
+    for c in range(chunks):
+        gain_ref[tile_rows(c), :] = by_mode(lambda m: gain_in[m], c)
+        factors = [by_mode(lambda m: terms_ref[k, m], c) for k in range(3)]
+
+        def spread(tile, carry):
+            bins = me + count * (tile * LANES + lane)
+            signed = jnp.where(bins < total_count // 2, bins, bins - total_count)
+            angular = signed.astype(jnp.float32) * (2.0 / total_count)
+            square = angular * angular
+            phase = (
+                factors[0] * angular + factors[1] * square / 2 + factors[2] * (square * angular) / 6
+            )
+            sine, cosine = sine_cosine(phase)
+            lanes = pl.ds(pl.multiple_of(tile * LANES, LANES), LANES)
+            spread_cos_ref[tile_rows(c), lanes] = cosine
+            spread_sin_ref[tile_rows(c), lanes] = sine
+            return carry
+
+        lax.fori_loop(0, width // 2, spread, 0, unroll=4)
 
     def columns_out(source, dst, ex, c):
         at = tile_rows(c)
         items = short_fft([source[a, at, :] for a in range(count)], -1.0, sgn)
         for d, value in enumerate(items):
             dst[d, at, :] = packed_mul(value, twist_cos_ref[d : d + 1, :], twist_sin_ref[d : d + 1, :])
-        post(dst, ex, c)
+        post(block_of(dst), ex, c)
 
     def row_in(ex, c):
         at = tile_rows(c)
@@ -344,7 +454,11 @@
 
     def row_out(dst, ex, c):
         at = tile_rows(c)
-        by_size(c, lambda size: mix(c, size))
+        if modes % SUB == 0:
+            mix(c, SUB)
+        else:
+            pl.when(c < chunks - 1)(lambda: mix(c, SUB))
+            pl.when(c == chunks - 1)(lambda: mix(c, modes % SUB))
         items = []
         for tile in range(width // 2):
             lanes = pl.ds(tile * LANES, LANES)
@@ -360,15 +474,15 @@
             spec[p] = packed_mul(value, tw_cos_ref[p : p + 1, :], -tw_sin_ref[p : p + 1, :])
         block = spec[...].reshape(count * SUB, LANES)
         dst[:, at, :] = long_dft(block, inv_ref[...]).reshape(count, SUB, LANES)
-        post(dst, ex, c)
+        post(block_of(dst), ex, c)
 
     def columns_in(ex, c):
         at = tile_rows(c)
         items = [
             packed_mul(
                 recv[ex, d, at, :],
-                twist_cos_ref[d : d + 1, :] * scale,
-                twist_sin_ref[d : d + 1, :] * -scale,
+                twist_cos_ref[d : d + 1, :],
+                -twist_sin_ref[d : d + 1, :],
             )
             for d in range(count)
         ]
@@ -377,26 +491,37 @@
             acc[a] = acc[a] + value * value
 
     def power():
-        def body(a, carry):
-            part = jnp.sum(acc[a], axis=0, keepdims=True)
-            acc[a] = jnp.broadcast_to(2.0 * (part + swap(part)), (SUB, LANES))
+        def body(k, carry):
+            at = pl.ds(k * SUB, SUB)
+            part = jnp.sum(acc[at], axis=1, keepdims=True)
+            acc[at] = jnp.broadcast_to(2.0 * (part + swap(part)), (SUB, SUB, LANES))
             return carry
 
-        lax.fori_loop(0, count, body, 0, unroll=4)
+        lax.fori_loop(0, count // SUB, body, 0)
 
     def kerr(target, c):
         at = tile_rows(c)
         gain = gain_ref[at, :]
 
-        def body(a, carry):
-            x = field[a, at, :]
-            square = x * x
-            magnitude = square + swap(square)
-            sine, cosine = sine_cosine(gain * (acc[a] - magnitude))
-            target[a, at, :] = packed_mul(x, cosine, sine * sgn)
+        def body(k, carry):
+            first, second = pl.ds(k * SUB, SUB // 2), pl.ds(k * SUB + SUB // 2, SUB // 2)
+            values, angles = [], []
+            for part in (first, second):
+                x = field[part, at, :]
+                square = x * x
+                values.append(x)
+                angles.append(acc[part] - (square + swap(square)))
+            sine, cosine = sine_cosine(gain * jnp.where(low, angles[0], angles[1]))
+            other_sine, other_cosine = swap(sine), swap(cosine)
+            pairs = (
+                (jnp.where(low, cosine, other_cosine), jnp.where(low, -sine, other_sine)),
+                (jnp.where(low, other_cosine, cosine), jnp.where(low, -other_sine, sine)),
+            )
+            for part, x, (cosines, sines) in zip((first, second), values, pairs):
+                target[part, at, :] = packed_mul(x, cosines, sines)
             return carry
 
-        lax.fori_loop(0, count, body, 0, unroll=4)
+        lax.fori_loop(0, count // SUB, body, 0)
 
     ex = 1
     for repeat in range(STEPS):
@@ -438,50 +563,61 @@
 
     def finish(c):
         kerr(send.at[ex - 1], c)
-        post(send.at[ex - 1], ex, c)
+        post(block_of(send.at[ex - 1]), ex, c)
 
     each(finish)
 
-    def result(c):
+    for c in range(chunks):
         arrive(ex, c)
-        out_ref[:, tile_rows(c), :] = recv[ex, :, tile_rows(c), :]
-
-    each(result)
+        repack(2 * c)
+        if 4 * (2 * c + 1) < modes:
+            repack(2 * c + 1)
     for ex in range(exchanges):
-        sent = recv.at[ex, pl.ds(0, count - 1), pl.ds(0, modes)]
+        sent = send.at[0, pl.ds(0, count - 1), pl.ds(0, modes)]
         remote(sent, sent, ex, 0, (me + 1) % count).wait_send()
 
 
-def mega(x, coupling, spread_cos, spread_sin, tw_cos, tw_sin, twist_cos, twist_sin, gain, fwd, inv, modes, scale):
-    count, rows = x.shape[0], x.shape[1]
-    width = coupling.shape[2]
+def mega(pulses, coupling, terms, gain, tw_cos, tw_sin, fwd, inv, count, scale):
+    modes, width = coupling.shape[0], coupling.shape[2]
+    rows = -(-modes // SUB) * SUB
     pitch = width + SUB
     exchanges = 2 * STEPS + 2
-    chunks = rows // SUB
     vmem = pl.BlockSpec(memory_space=pltpu.VMEM)
+    smem = pl.BlockSpec(memory_space=pltpu.SMEM)
     block = (count, rows, LANES)
+    tiles = rows // SUB
+    groups = GROUPS if tiles == 4 else ((0, tiles),)
+    flat = (count * (rows + SUB), LANES)
+    mixed = (rows * pitch, LANES)
     return pl.pallas_call(
-        functools.partial(mega_kernel, count, modes, scale),
-        out_shape=jax.ShapeDtypeStruct(x.shape, x.dtype),
-        in_specs=[vmem, pl.BlockSpec(memory_space=pl.ANY)] + [vmem] * 9,
+        functools.partial(mega_kernel, count, modes, scale, groups),
+        out_shape=jax.ShapeDtypeStruct(pulses.shape, pulses.dtype),
+        in_specs=[vmem, pl.BlockSpec(memory_space=pl.ANY), smem, smem] + [vmem] * 4,
         out_specs=vmem,
         scratch_shapes=[
             pltpu.VMEM(coupling.shape, jnp.float32),
-            pltpu.VMEM((exchanges,) + block, jnp.float32),
+            pltpu.VMEM(flat, jnp.float32),
+            pltpu.VMEM((exchanges - 1,) + block, jnp.float32),
+            pltpu.VMEM(flat, jnp.float32),
             pltpu.VMEM((exchanges - 1,) + block, jnp.float32),
             pltpu.VMEM((count, SUB, LANES), jnp.float32),
-            pltpu.VMEM((rows * pitch, LANES), jnp.float32),
-            pltpu.VMEM((rows * pitch, LANES), jnp.float32),
+            pltpu.VMEM(mixed, jnp.float32),
+            pltpu.VMEM(mixed, jnp.float32),
             pltpu.VMEM((SUB * pitch, LANES), jnp.float32),
             pltpu.VMEM(block, jnp.float32),
             pltpu.VMEM((count, SUB, LANES), jnp.float32),
+            pltpu.VMEM((rows, width // 2 * LANES), jnp.float32),
+            pltpu.VMEM((rows, width // 2 * LANES), jnp.float32),
+            pltpu.VMEM((count, LANES), jnp.float32),
+            pltpu.VMEM((count, LANES), jnp.float32),
+            pltpu.VMEM((rows, LANES), jnp.float32),
             pltpu.SemaphoreType.DMA((exchanges,)),
-            pltpu.SemaphoreType.DMA((exchanges, chunks)),
+            pltpu.SemaphoreType.DMA((exchanges, len(groups))),
             pltpu.SemaphoreType.DMA(()),
         ],
         compiler_params=pltpu.CompilerParams(collective_id=0, has_side_effects=True),
         name="mega",
-    )(x, coupling, spread_cos, spread_sin, tw_cos, tw_sin, twist_cos, twist_sin, gain, fwd, inv)
+    )(pulses, coupling, terms, gain, tw_cos, tw_sin, fwd, inv)
 
 
 def packed_table(cosine, sine):
@@ -492,10 +628,17 @@
     )
 
 
-def dft_weights(size, orient):
-    index = np.arange(size)
-    angle = orient * 2.0 * np.pi * (index[:, None] * index[None, :] % size) / size
-    cosine, sine = np.cos(angle), np.sin(angle)
+def lane_order(size):
+    place = np.arange(size)
+    return place % ROW * (size // ROW) + place // ROW
+
+
+def dft_weights(size, orient, scale):
+    first, second = lane_order(size), np.arange(size)
+    if orient > 0:
+        first, second = second, first
+    angle = orient * 2.0 * np.pi * (first[:, None] * second[None, :] % size) / size
+    cosine, sine = scale * np.cos(angle), scale * np.sin(angle)
     full = np.block([[cosine, sine], [-sine, cosine]]).astype(np.float32)
     high = full.astype(jnp.bfloat16)
     low = (full - high.astype(np.float32)).astype(jnp.bfloat16)
@@ -504,43 +647,20 @@
 
 def packed_device(pulses, coupling, dispersion_terms, kerr_gain):
     shards = lax.axis_size("freq")
-    device = lax.axis_index("freq")
     modes, local = pulses.shape[2], pulses.shape[3]
     groups = local // shards
-    total = local * shards
-    rows = -(-modes // SUB) * SUB
-    pad = rows - modes
+    tiles = local // LANES
+    scale = 1.0 / (local * shards)
 
     shard_index = np.arange(shards)
     angle = -2.0 * np.pi * (shard_index[:, None] * np.arange(groups)[None, :] % local) / local
     tw_cos, tw_sin = packed_table(np.cos(angle), np.sin(angle))
-    fwd, inv = dft_weights(groups, -1.0), dft_weights(groups, 1.0)
-    samples = device + shards * jnp.arange(groups, dtype=jnp.int32)
-    twist_cos, twist_sin = packed_table(
-        *angle_table(jnp.arange(shards, dtype=jnp.int32), samples, total, -1.0)
-    )
-    gain = jnp.broadcast_to(jnp.pad(kerr_gain, (0, pad))[:, None], (rows, LANES))
-
-    bins = device + shards * jnp.arange(local, dtype=jnp.int32)
-    signed_bin = jnp.where(bins < total // 2, bins, bins - total).astype(jnp.float32)
-    angular = signed_bin / (total // 2)
-    terms = jnp.pad(dispersion_terms, ((0, 0), (0, pad)))
-    dispersion = (
-        terms[0][:, None] * angular
-        + terms[1][:, None] * angular**2 / 2
-        + terms[2][:, None] * angular**3 / 6
-    )
-    spread_cos, spread_sin = jnp.cos(dispersion), jnp.sin(dispersion)
-
-    coupling = coupling.reshape(2, modes, modes, local // LANES, LANES).transpose(1, 2, 3, 0, 4)
-    coupling = coupling.reshape(modes, modes, 2 * local // LANES, LANES)
-    blocks = pulses.reshape(2, modes, groups, shards).transpose(3, 1, 0, 2)
-    x = jnp.pad(blocks.reshape(shards, modes, 2 * groups), ((0, 0), (0, pad), (0, 0)))
-    scale = 1.0 / total
-    x = mega(
-        x, coupling, spread_cos, spread_sin, tw_cos, tw_sin, twist_cos, twist_sin, gain, fwd, inv, modes, scale
-    )
-    x = x[:, :modes].reshape(shards, modes, 2, groups).transpose(2, 1, 3, 0)
+    fwd, inv = dft_weights(groups, -1.0, 1.0), dft_weights(groups, 1.0, scale)
+    coupling = coupling.reshape(2, modes, modes, tiles, LANES).transpose(1, 2, 3, 0, 4)
+    coupling = coupling.reshape(modes, modes, 2 * tiles, LANES)
+    x = pulses.reshape(2, modes, tiles, LANES).transpose(1, 2, 0, 3).reshape(modes, 2 * tiles, LANES)
+    x = mega(x, coupling, dispersion_terms, kerr_gain, tw_cos, tw_sin, fwd, inv, shards, scale)
+    x = x.reshape(modes, tiles, 2, LANES).transpose(2, 0, 1, 3)
     return x.reshape(1, 2, modes, local)
 
 
@@ -549,7 +669,7 @@
     return (
         pulses.shape[0] == 1
         and shards & (shards - 1) == 0
-        and shards >= 4
+        and shards == 2 * ROW
         and local == shards * HALF
     )
 

time: 105 us -> 96.2 us (0.916)
  local copies, waits for them, and re-layouts: 8.63 us -> 1.84 us
  other arithmetic: 2.67 us -> 0 us
    reshape x4 -> x0, local copies, waits for them, and re-layouts: 4.99 us -> none  [the longest x1 1.87 us: packed_device(): blocks = pulses.reshape(2, modes, groups, shards).transpose(3, 1, 0, 2)]
    sin x1 -> x0, other arithmetic: 1.86 us -> none  [packed_device(): spread_cos, spread_sin = (jnp.cos(dispersion), jnp.sin(dispersion))]
    unnamed x4 -> x1, local copies, waits for them, and re-layouts: 0.01 us -> 1.84 us
    slice x1 -> x0, local copies, waits for them, and re-layouts: 1.33 us -> none  [packed_device(): x = x[:, :modes].reshape(shards, modes, 2, groups).transpose(2, 1, 3, 0)]
where the time goes in v2:
time: 96.2 us; the launch traced here: 96 us
  Pallas kernels  94.2 us (98%)
  local copies, waits for them, and re-layouts  1.84 us (2%)
    pallas_call x1, Pallas kernels, mega(): pl.pallas_call(functools.partial(mega_kernel, count, modes, scale, groups...  94.2 us

profile of v2, /device:TPU:0, one launch (start us, length us, event | category | flops | bytes accessed | tf_op | source)
XLA Modules:
  0.0 96.0 jit_solution(8140568214162102860)
XLA Ops:
  0.0 94.2 %mega.1 = f32[30,32,128]{2,1,0:T(8,128)} custom-call(f32[30,32,128]{2,1,0:T(8,128)} %bitcast.17, f32[30,30,32,128]{3,2,1,0:T(8,128)} %bitcast.15, f32[3,30]{1,0:T(4,128)} %terms_ref.1, f32[30]{0:T(128)} %gain_in.1, f32[32,128]{1,0:T(8,128)} %constant.8.clone.tw_cos_ref, f32[32,128]{1,0:T(8,128)} %constant.9.clone.tw_sin_ref, ...), custom_call_target="tpu_custom_call" | custom-call | tf_op jit(solution)/shard_map/mega/pallas_call | solution.py:592
  94.2 1.8 %copy.13 = f32[1,2,30,2048]{3,1,2,0:T(2,128)} copy(f32[1,2,30,2048]{3,1,2,0:T(2,128)} %bitcast.16) | data formatting | bytes 983040

commit v3 on v2

--- a/solution.py
+++ b/solution.py
@@ -123,7 +123,8 @@
 HALF = LANES // 2
 SUB = 8
 ROW = 16
-GROUPS = ((0, 1), (1, 3), (3, 4))
+CLASSES = 2
+GROUPS = (((0, 1), (1, 2), (2, 3), (3, 4)),) * 6
 
 
 def low_lanes(shape):
@@ -218,12 +219,25 @@
 
 
 def mega_kernel(
-    count, modes, scale, groups, pulse_ref, c_hbm, terms_ref, gain_in, tw_cos_ref, tw_sin_ref,
-    fwd_ref, inv_ref, out_ref, c_ref, early, recv, late, send, spec, by_real, by_imag, total, field,
+    count, modes, scale, groups, pulse_hbm, c_hbm, terms_ref, gain_in, tw_cos_ref, tw_sin_ref,
+    fwd_ref, inv_ref, out_ref, pulse_ref, c_ref, early, recv, late, send, spec, by_real, by_imag, total, field,
     acc, spread_cos_ref, spread_sin_ref, twist_cos_ref, twist_sin_ref, gain_ref,
     send_sem, recv_sem, c_sem,
 ):
     me = lax.axis_index("freq")
+    barrier = pltpu.get_barrier_semaphore()
+
+    def greet(k, carry):
+        pl.semaphore_signal(
+            barrier, inc=1, device_id=((me + k) % count,), device_id_type=pl.DeviceIdType.MESH
+        )
+        return carry
+
+    lax.fori_loop(1, count, greet, 0)
+    fetch = pltpu.make_async_copy(pulse_hbm, pulse_ref, c_sem.at[0])
+    fetch.start()
+    load = pltpu.make_async_copy(c_hbm, c_ref, c_sem.at[1])
+    load.start()
     chunks = recv.shape[2] // SUB
     rows = recv.shape[2]
     width = c_ref.shape[2]
@@ -234,6 +248,22 @@
     odd = lax.broadcasted_iota(jnp.int32, (SUB, LANES), 0) % 2 == 1
     exchanges = recv.shape[0] + 1
 
+    near = 8
+    outer_peers = []
+    for k in reversed(range(count // near)):
+        place = 0
+        for b in range((count // near).bit_length() - 1):
+            place = place + ((me // (near << b) + (k >> b)) % 2) * (near << b)
+        outer_peers.append(place)
+    own_low = me % CLASSES
+    step_bits = [(me // (CLASSES << b)) % 2 for b in range((near // CLASSES).bit_length() - 1)]
+
+    def inner_peer(j):
+        place = 0
+        for b, mine in enumerate(step_bits):
+            place = place + ((j // (1 << b) + mine) % 2) * (CLASSES << b)
+        return place
+
     def tile_rows(c):
         return pl.ds(pl.multiple_of(c * SUB, SUB), SUB)
 
@@ -256,34 +286,47 @@
             device_id_type=pl.DeviceIdType.MESH,
         )
 
-    def extent(g):
-        start, end = groups[g]
+    def extent(ex, g):
+        start, end = groups[ex][g]
         return start * SUB, min(end * SUB, modes) - start * SUB
 
-    def post(src, ex, c):
+    def post(src, ex, c, kind):
         dst = landing(ex)
-        for g, (_, end) in enumerate(groups):
-            row, size = extent(g)
+        for g, (_, end) in enumerate(groups[ex]):
+            row, size = extent(ex, g)
 
             def go(row=row, size=size, g=g):
-                dst(me, row, size)[...] = src(me, row, size)[...]
-
-                def one(j, carry):
-                    k = count - j
-                    peer = 0
-                    for b in range(count.bit_length() - 1):
-                        mine = (me // (1 << b)) % 2
-                        peer = peer + ((k // (1 << b) + mine) % 2) * (1 << b)
+                def one(peer):
                     remote(src(peer, row, size), dst(me, row, size), ex, g, peer).start()
+
+                def several(j, carry):
+                    inner = inner_peer(near // CLASSES - j)
+                    for outer in outer_peers:
+                        one(outer + inner + kind)
                     return carry
 
-                lax.fori_loop(1, count, one, 0)
+                lax.fori_loop(1, near // CLASSES, several, 0)
+                inner = inner_peer(0)
+                for outer in outer_peers[:-1]:
+                    one(outer + inner + kind)
+                pl.when(own_low != kind)(lambda: one(outer_peers[-1] + inner + kind))
+
+                @pl.when(own_low == kind)
+                def _():
+                    dst(me, row, size)[...] = src(me, row, size)[...]
 
             pl.when(c == end - 1)(go)
 
+    def post_rest(src, ex):
+        def body(i, carry):
+            post(src, ex, i % chunks, 1 + i // chunks)
+            return carry
+
+        lax.fori_loop(0, chunks * (CLASSES - 1), body, 0)
+
     def arrive(ex, c):
-        for g, (start, _) in enumerate(groups):
-            row, size = extent(g)
+        for g, (start, _) in enumerate(groups[ex]):
+            row, size = extent(ex, g)
 
             def go(row=row, size=size, g=g):
                 if ex == exchanges - 1:
@@ -301,22 +344,10 @@
 
         lax.fori_loop(0, chunks, step, 0)
 
-    load = pltpu.make_async_copy(c_hbm, c_ref, c_sem)
-    load.start()
-    barrier = pltpu.get_barrier_semaphore()
-
-    def greet(k, carry):
-        pl.semaphore_signal(
-            barrier, inc=1, device_id=((me + k) % count,), device_id_type=pl.DeviceIdType.MESH
-        )
-        return carry
-
-    lax.fori_loop(1, count, greet, 0)
     if rows > modes:
         spare = pl.ds(modes, rows - modes)
         for ex in range(exchanges - 1):
             recv[ex, :, spare, :] = jnp.zeros((count, rows - modes, LANES), jnp.float32)
-    total[...] = jnp.zeros_like(total)
 
     def unpack(q):
         names = [min(4 * q + i, modes - 1) for i in range(4)]
@@ -352,15 +383,12 @@
                             at : at + SUB
                         ]
 
-    for q in range(2 * groups[0][1]):
+    fetch.wait()
+    for q in range(-(-modes // 4)):
         unpack(q)
     pl.semaphore_wait(barrier, count - 1)
-    for c in range(chunks):
-        if c >= groups[0][1]:
-            unpack(2 * c)
-            unpack(2 * c + 1)
-        if c in [end - 1 for _, end in groups]:
-            post(flat_of(early), 0, c)
+    each(lambda c: post(flat_of(early), 0, c, 0))
+    post_rest(flat_of(early), 0)
 
     lane = lax.broadcasted_iota(jnp.int32, (SUB, LANES), 1)
     line = lax.broadcasted_iota(jnp.int32, (SUB, LANES), 0)
@@ -398,13 +426,14 @@
             return carry
 
         lax.fori_loop(0, width // 2, spread, 0, unroll=4)
-
-    def columns_out(source, dst, ex, c):
+    total[...] = jnp.zeros_like(total)
+
+    def columns_out(source, where, dst, ex, c):
         at = tile_rows(c)
-        items = short_fft([source[a, at, :] for a in range(count)], -1.0, sgn)
+        items = short_fft([source[a, where, :] for a in range(count)], -1.0, sgn)
         for d, value in enumerate(items):
             dst[d, at, :] = packed_mul(value, twist_cos_ref[d : d + 1, :], twist_sin_ref[d : d + 1, :])
-        post(block_of(dst), ex, c)
+        post(block_of(dst), ex, c, 0)
 
     def row_in(ex, c):
         at = tile_rows(c)
@@ -474,7 +503,7 @@
             spec[p] = packed_mul(value, tw_cos_ref[p : p + 1, :], -tw_sin_ref[p : p + 1, :])
         block = spec[...].reshape(count * SUB, LANES)
         dst[:, at, :] = long_dft(block, inv_ref[...]).reshape(count, SUB, LANES)
-        post(block_of(dst), ex, c)
+        post(block_of(dst), ex, c, 0)
 
     def columns_in(ex, c):
         at = tile_rows(c)
@@ -499,12 +528,13 @@
 
         lax.fori_loop(0, count // SUB, body, 0)
 
-    def kerr(target, c):
+    def kerr(target, c, to):
         at = tile_rows(c)
         gain = gain_ref[at, :]
 
-        def body(k, carry):
-            first, second = pl.ds(k * SUB, SUB // 2), pl.ds(k * SUB + SUB // 2, SUB // 2)
+        half = SUB // 2
+        for k in range(count // SUB):
+            first, second = pl.ds(k * SUB, half), pl.ds(k * SUB + half, half)
             values, angles = [], []
             for part in (first, second):
                 x = field[part, at, :]
@@ -518,10 +548,7 @@
                 (jnp.where(low, other_cosine, cosine), jnp.where(low, -other_sine, sine)),
             )
             for part, x, (cosines, sines) in zip((first, second), values, pairs):
-                target[part, at, :] = packed_mul(x, cosines, sines)
-            return carry
-
-        lax.fori_loop(0, count // SUB, body, 0)
+                target[part, to, :] = packed_mul(x, cosines, sines)
 
     ex = 1
     for repeat in range(STEPS):
@@ -530,17 +557,19 @@
 
             def begin(c):
                 arrive(0, c)
-                columns_out(recv.at[0], dst, ex, c)
+                columns_out(recv.at[0], tile_rows(c), dst, ex, c)
 
             each(begin)
+            post_rest(block_of(dst), ex)
         else:
             power()
 
             def bend(c):
-                kerr(field, c)
-                columns_out(field, dst, ex, c)
+                kerr(spec, c, pl.ds(0, SUB))
+                columns_out(spec, pl.ds(0, SUB), dst, ex, c)
 
             each(bend)
+            post_rest(block_of(dst), ex)
 
         def inward(c):
             arrive(ex, c)
@@ -551,6 +580,7 @@
             load.wait()
         ex += 1
         each(lambda c: row_out(send.at[ex - 1], ex, c))
+        post_rest(block_of(send.at[ex - 1]), ex)
         acc[...] = jnp.zeros_like(acc)
 
         def collect(c):
@@ -562,10 +592,11 @@
     power()
 
     def finish(c):
-        kerr(send.at[ex - 1], c)
-        post(block_of(send.at[ex - 1]), ex, c)
+        kerr(send.at[ex - 1], c, tile_rows(c))
+        post(block_of(send.at[ex - 1]), ex, c, 0)
 
     each(finish)
+    post_rest(block_of(send.at[ex - 1]), ex)
 
     for c in range(chunks):
         arrive(ex, c)
@@ -586,15 +617,16 @@
     smem = pl.BlockSpec(memory_space=pltpu.SMEM)
     block = (count, rows, LANES)
     tiles = rows // SUB
-    groups = GROUPS if tiles == 4 else ((0, tiles),)
+    groups = GROUPS if tiles == 4 else (((0, tiles),),) * exchanges
     flat = (count * (rows + SUB), LANES)
     mixed = (rows * pitch, LANES)
     return pl.pallas_call(
         functools.partial(mega_kernel, count, modes, scale, groups),
         out_shape=jax.ShapeDtypeStruct(pulses.shape, pulses.dtype),
-        in_specs=[vmem, pl.BlockSpec(memory_space=pl.ANY), smem, smem] + [vmem] * 4,
+        in_specs=[pl.BlockSpec(memory_space=pl.ANY)] * 2 + [smem, smem] + [vmem] * 4,
         out_specs=vmem,
         scratch_shapes=[
+            pltpu.VMEM(pulses.shape, jnp.float32),
             pltpu.VMEM(coupling.shape, jnp.float32),
             pltpu.VMEM(flat, jnp.float32),
             pltpu.VMEM((exchanges - 1,) + block, jnp.float32),
@@ -612,8 +644,8 @@
             pltpu.VMEM((count, LANES), jnp.float32),
             pltpu.VMEM((rows, LANES), jnp.float32),
             pltpu.SemaphoreType.DMA((exchanges,)),
-            pltpu.SemaphoreType.DMA((exchanges, len(groups))),
-            pltpu.SemaphoreType.DMA(()),
+            pltpu.SemaphoreType.DMA((exchanges, tiles)),
+            pltpu.SemaphoreType.DMA((2,)),
         ],
         compiler_params=pltpu.CompilerParams(collective_id=0, has_side_effects=True),
         name="mega",

time: 96.2 us -> 86.6 us (0.900)
  Pallas kernels: 94.2 us -> 83.8 us
    pallas_call x1, Pallas kernels: 94.2 us -> 83.8 us  [mega(): pl.pallas_call(functools.partial(mega_kernel, count, modes, scale, groups...]
where the time goes in v3:
time: 86.6 us; the launch traced here: 85.6 us
  Pallas kernels  83.8 us (97%)
  local copies, waits for them, and re-layouts  1.84 us (2%)
    pallas_call x1, Pallas kernels, mega(): pl.pallas_call(functools.partial(mega_kernel, count, modes, scale, groups...  83.8 us
    unnamed x1, local copies, waits for them, and re-layouts  1.84 us

profile of v3, /device:TPU:0, one launch (start us, length us, event | category | flops | bytes accessed | tf_op | source)
XLA Modules:
  0.0 85.6 jit_solution(13246557078026292573)
XLA Ops:
  0.0 83.8 %mega.1 = f32[30,32,128]{2,1,0:T(8,128)} custom-call(f32[30,32,128]{2,1,0:T(8,128)} %bitcast.17, f32[30,30,32,128]{3,2,1,0:T(8,128)} %bitcast.15, f32[3,30]{1,0:T(4,128)} %terms_ref.1, f32[30]{0:T(128)} %gain_in.1, f32[32,128]{1,0:T(8,128)} %constant.8.clone.tw_cos_ref, f32[32,128]{1,0:T(8,128)} %constant.9.clone.tw_sin_ref, ...), custom_call_target="tpu_custom_call" | custom-call | tf_op jit(solution)/shard_map/mega/pallas_call | solution.py:623
  83.8 1.8 %copy.13 = f32[1,2,30,2048]{3,1,2,0:T(2,128)} copy(f32[1,2,30,2048]{3,1,2,0:T(2,128)} %bitcast.16) | data formatting | bytes 983040

commit v4 on v3

--- a/solution.py
+++ b/solution.py
@@ -124,7 +124,14 @@
 SUB = 8
 ROW = 16
 CLASSES = 2
-GROUPS = (((0, 1), (1, 2), (2, 3), (3, 4)),) * 6
+GROUPS = (
+    ((0, 2), (2, 4)),
+    ((0, 1), (1, 2), (2, 3), (3, 4)),
+    ((0, 1), (1, 2), (2, 3), (3, 4)),
+    ((0, 1), (1, 2), (2, 3), (3, 4)),
+    ((0, 1), (1, 2), (2, 3), (3, 4)),
+    ((0, 2), (2, 3), (3, 4)),
+)
 
 
 def low_lanes(shape):

time: 86.6 us -> 86.7 us (level)
  no operation moved by 1% of the time
where the time goes in v4:
time: 86.7 us; the launch traced here: 85.9 us
  Pallas kernels  84.1 us (97%)
  local copies, waits for them, and re-layouts  1.84 us (2%)
    pallas_call x1, Pallas kernels, mega(): pl.pallas_call(functools.partial(mega_kernel, count, modes, scale, groups...  84.1 us
    unnamed x1, local copies, waits for them, and re-layouts  1.84 us

profile of v4, /device:TPU:0, one launch (start us, length us, event | category | flops | bytes accessed | tf_op | source)
XLA Modules:
  0.0 85.9 jit_solution(6920035155707565754)
XLA Ops:
  0.0 84.1 %mega.1 = f32[30,32,128]{2,1,0:T(8,128)} custom-call(f32[30,32,128]{2,1,0:T(8,128)} %bitcast.17, f32[30,30,32,128]{3,2,1,0:T(8,128)} %bitcast.15, f32[3,30]{1,0:T(4,128)} %terms_ref.1, f32[30]{0:T(128)} %gain_in.1, f32[32,128]{1,0:T(8,128)} %constant.8.clone.tw_cos_ref, f32[32,128]{1,0:T(8,128)} %constant.9.clone.tw_sin_ref, ...), custom_call_target="tpu_custom_call" | custom-call | tf_op jit(solution)/shard_map/mega/pallas_call | solution.py:630
  84.1 1.8 %copy.13 = f32[1,2,30,2048]{3,1,2,0:T(2,128)} copy(f32[1,2,30,2048]{3,1,2,0:T(2,128)} %bitcast.16) | data formatting | bytes 983040
